TPU v7x, 512 devices: a whole 4x4x16 slice. The times are simulated.
512 devices in a mesh: section: 8 (over x, core), expert: 64 (over y, z).
Axes of the slice: x: 4, y: 4, z: 16, core: 2. Of those that a mesh axis runs over, the one named last changes fastest.
Arguments:
- images: bfloat16 [512, 256, 1408], P(('section', 'expert')), may hold values from -6 to 6
- norm_gain: bfloat16 [1408], replicated, may hold values from 0.5 to 1.5
- slot_map: bfloat16 [1408, 64], replicated, may hold values from -0.15625 to 0.15625
- logit_scale: float32 [1], replicated, may hold values from 30 to 80
- up_weight: bfloat16 [64, 5120, 1408], P('expert', 'section'), may hold values from -0.625 to 0.625
- down_weight: bfloat16 [64, 5120, 1408], P('expert', 'section'), may hold values from -0.3125 to 0.3125
Outputs:
- block_out: bfloat16 [512, 256, 1408], P(('section', 'expert'))
All inputs are finite; a program needn't handle non-finite values.
Results may differ from a plain program's by a relative error of at most 0.011.
Values may be sent and summed in bfloat16 or wider, within the bound.
A program may use at most 64 MiB of HBM per device.

v0:
```python
import jax
import jax.numpy as jnp
from jax import lax
from jax.sharding import PartitionSpec as P

epsilon = 1e-06


def sent_to_all(array, axis):
    copies = jnp.broadcast_to(array, (lax.axis_size(axis), *array.shape))
    return lax.all_to_all(copies, axis, split_axis=0, concat_axis=0, tiled=True)


def joined_along(parts, dim):
    lengths = list(parts.shape[1:])
    lengths[dim] *= parts.shape[0]
    return jnp.moveaxis(parts, 0, dim).reshape(lengths)


def gathered_copies(array, axis, dim):
    parts = sent_to_all(array, axis)
    return joined_along(parts, dim)


def cut_along(array, dim, peers):
    lengths = array.shape
    parts = array.reshape(*lengths[:dim], peers, lengths[dim] // peers, *lengths[dim + 1 :])
    return jnp.moveaxis(parts, dim, 0)


def summed_on_arrival(array, axis, dim):
    peers = lax.axis_size(axis)
    parts = lax.all_to_all(cut_along(array, dim, peers), axis, 0, 0, tiled=True)
    return jnp.sum(parts, axis=0)


def normalize(inputs, gain_row):
    values = inputs.astype(jnp.float32)
    spread = jnp.mean(values * values, axis=-1, keepdims=True)
    return (values * lax.rsqrt(spread + epsilon) * gain_row.astype(jnp.float32)).astype(
        jnp.bfloat16
    )


def weights_from(raw, normed, slot_cols, scale_now):
    values = normed.astype(jnp.float32)
    token_norm = jnp.sqrt(jnp.sum(values * values, axis=-1) + epsilon)
    columns = slot_cols.astype(jnp.float32)
    column_norm = jnp.sqrt(jnp.sum(columns * columns, axis=0) + epsilon)
    logits = scale_now * raw / (token_norm[:, None, :] * column_norm[None, :, None])
    scores = jnp.exp(logits)
    dispatch = (scores / jnp.sum(scores, axis=-1, keepdims=True)).astype(jnp.bfloat16)
    combine = (scores / jnp.sum(scores, axis=1, keepdims=True)).astype(jnp.bfloat16)
    return (dispatch, combine)


def local(images, norm_gain, slot_map, logit_scale, up_weight, down_weight):
    normed = normalize(images, norm_gain)
    raw = jnp.einsum("itd,de->iet", normed, slot_map, preferred_element_type=jnp.float32)
    dispatch, combine = weights_from(raw, normed, slot_map, logit_scale[0])
    slot_in = jnp.einsum(
        "iet,itd->eid", dispatch, normed, preferred_element_type=jnp.float32
    ).astype(jnp.bfloat16)
    gathered = gathered_copies(
        lax.all_to_all(slot_in, "expert", split_axis=0, concat_axis=1, tiled=True), "section", 1
    )
    hidden = jax.nn.gelu(
        jnp.einsum("esd,efd->esf", gathered, up_weight, preferred_element_type=jnp.float32)
    ).astype(jnp.bfloat16)
    partial_sum = jnp.einsum(
        "esf,efd->esd", hidden, down_weight, preferred_element_type=jnp.float32
    )
    own_rows = summed_on_arrival(partial_sum, "section", 1)
    result = own_rows.astype(jnp.bfloat16)
    back = lax.all_to_all(result, "expert", split_axis=1, concat_axis=0, tiled=True)
    mixed = jnp.einsum("iet,eid->itd", combine, back, preferred_element_type=jnp.float32)
    return (images.astype(jnp.float32) + mixed).astype(jnp.bfloat16)


def solution(mesh):
    return jax.shard_map(
        local,
        mesh=mesh,
        in_specs=(
            P(("section", "expert"), None, None),
            P(),
            P(),
            P(),
            P("expert", "section", None),
            P("expert", "section", None),
        ),
        out_specs=P(("section", "expert"), None, None),
        check_vma=False,
    )
```

profile of v0, /device:TPU:1, one launch (start us, length us, event | category | flops | bytes accessed | tf_op | source)
XLA Modules:
  0.0 139.3 jit_solution(4139029451636734264)
XLA Ops:
  0.0 0.0 copy-start
  0.0 0.0 copy-start.2
  0.0 0.0 copy-start.1
  0.8 1.1 multiply_reduce_fusion.1
  1.9 1.3 fusion.6
  3.3 0.7 convert_element_type.55
  4.0 1.5 %multiply_reduce_fusion = f32[256]{0:T(256)S(1)} fusion(f32[1408]{0:T(1024)S(1)} %convert_element_type.55, f32[256]{0:T(256)S(1)} %add_rsqrt_fusion, bf16[1,256,1408]{2,1,0:T(8,128)(2,1)} %param.6), kind=kLoop, calls=%fused_computation.15 | loop fusion | flops 2522880 | bytes 728576 | tf_op jit(solution)/shard_map/reduce_sum | solution.py:47
  5.5 0.0 copy-done.2
  5.5 0.0 copy-done.1
  5.5 0.5 fusion.30
  6.0 0.4 fusion.2
  6.4 0.5 broadcast.42
  6.9 0.7 reduce.7
  7.6 0.2 reshape.125
  7.8 35.8 %all_to_all.31 = bf16[64,2,704]{2,1,0:T(2,128)(2,1)S(1)} all-to-all(bf16[64,2,704]{2,1,0:T(2,128)(2,1)S(1)} %reshape.125), channel_id=1, replica_groups=mesh['section'=8,'expert'=64] {'expert'}, dimensions={0} | all-to-all | bytes 360448 | tf_op jit(solution)/shard_map/all_to_all | solution.py:65
  43.7 0.2 reshape.126
  43.9 0.1 broadcast_in_dim.2
  44.1 0.0 copy-start.3
  44.1 26.0 %all_to_all.32 = bf16[8,1,64,1408]{3,2,1,0:T(8,128)(2,1)S(1)} all-to-all(bf16[8,1,64,1408]{3,2,1,0:T(8,128)(2,1)S(1)} %broadcast_in_dim.2), channel_id=1, replica_groups=mesh['section'=8,'expert'=64] {'section'}, dimensions={0} | all-to-all | bytes 2883584 | tf_op jit(solution)/shard_map/all_to_all | solution.py:11
  70.0 0.0 copy-done.3
  70.1 1.4 %fusion.16 = bf16[512,640]{1,0:T(8,128)(2,1)S(1)} fusion(bf16[512,1408]{1,0:T(8,128)(2,1)S(1)} %bitcast.56, bf16[1,640,1408]{2,1,0:T(8,128)(2,1)S(1)} %copy-done.3), kind=kOutput, calls=%fused_computation.23 | convolution fusion | flops 925696000 | bytes 3899392 | tf_op jit(solution)/shard_map/esd,efd->esf/dot_general | solution.py:68
  71.5 0.0 copy-done
  71.5 1.3 convolution_bitcast_fusion
  72.9 38.7 %all_to_all.33 = f32[8,1,64,1408]{3,2,1,0:T(8,128)} all-to-all(f32[8,1,64,1408]{3,2,1,0:T(8,128)S(1)} %convolution_bitcast_fusion), channel_id=1, replica_groups=mesh['section'=8,'expert'=64] {'section'}, dimensions={0} | all-to-all | bytes 5767168 | tf_op jit(solution)/shard_map/all_to_all | solution.py:33
  111.5 2.0 %reduce_sum.59 = bf16[64,1408]{1,0:T(8,128)(2,1)S(1)} reduce(f32[8,1,64,1408]{3,2,1,0:T(8,128)} %all_to_all.33, f32[]{:T(128)} %constant.7.clone.1), dimensions={0,1}, to_apply=%region_5.0 | reduce | flops 630784 | bytes 3063812 | tf_op jit(solution)/shard_map/reduce_sum | solution.py:34
  113.5 0.3 copy.21
  113.8 1.7 %reduce.8 = bf16[64,1408]{1,0:T(8,128)(2,1)S(1)} reduce(bf16[64,1,1408]{2,1,0:T(2,128)(2,1)S(1)} %bitcast.57, bf16[]{:T(256)} %broadcast.42), dimensions={1}, to_apply=%bitcast.54.reduce_sub_computation | reduce | bytes 360450
  115.5 0.2 reshape.127
  115.7 22.1 %all_to_all.34 = bf16[64,2,704]{2,1,0:T(2,128)(2,1)S(1)} all-to-all(bf16[64,2,704]{2,1,0:T(2,128)(2,1)S(1)} %reshape.127), channel_id=1, replica_groups=mesh['section'=8,'expert'=64] {'expert'}, dimensions={0} | all-to-all | bytes 360448 | tf_op jit(solution)/shard_map/all_to_all | solution.py:75
  137.8 0.2 reshape.128
  138.0 1.2 fusion.1
  (4 shorter events, 0.0 us)
Async XLA Ops:
  0.0 71.5 %copy-start = (bf16[1,640,1408]{2,1,0:T(8,128)(2,1)S(1)}, bf16[1,640,1408]{2,1,0:T(8,128)(2,1)}, u32[]{:S(2)}) copy-start(bf16[1,640,1408]{2,1,0:T(8,128)(2,1)} %param.11) | copy-start | bytes 5406724
  0.0 5.5 %copy-start.2 = (bf16[1408,64]{0,1:T(8,128)(2,1)S(1)}, bf16[1408,64]{0,1:T(8,128)(2,1)}, u32[]{:S(2)}) copy-start(bf16[1408,64]{0,1:T(8,128)(2,1)} %param.8) | copy-start | bytes 540676
  0.0 5.5 %copy-start.1 = (bf16[1,256,1408]{2,1,0:T(8,128)(2,1)S(1)}, bf16[1,256,1408]{2,1,0:T(8,128)(2,1)}, u32[]{:S(2)}) copy-start(bf16[1,256,1408]{2,1,0:T(8,128)(2,1)} %param.6) | copy-start | bytes 2162692
  44.1 26.0 %copy-start.3 = (bf16[1,640,1408]{2,1,0:T(8,128)(2,1)S(1)}, bf16[1,640,1408]{2,1,0:T(8,128)(2,1)}, u32[]{:S(2)}) copy-start(bf16[1,640,1408]{2,1,0:T(8,128)(2,1)} %param.10) | copy-start | bytes 5406724
where the time goes:
time: 141 us; the launch traced here: 139 us
  blocking collectives  123 us (87%)
  other arithmetic  8.99 us (6%)
  matrix products  4.96 us (4%)
  local copies, waits for them, and re-layouts  1.82 us (1%)
    all_to_all x1, blocking collectives, summed_on_arrival(): parts = lax.all_to_all(cut_along(array, dim, peers), axis, 0, 0, tiled=True)  38.7 us
    all_to_all x1, blocking collectives, local(): lax.all_to_all(slot_in, 'expert', split_axis=0, concat_axis=1, tiled=True)  35.8 us
    all_to_all x1, blocking collectives, sent_to_all(): return lax.all_to_all(copies, axis, split_axis=0, concat_axis=0, tiled=True)  26 us
    all_to_all x1, blocking collectives, local(): lax.all_to_all(result, 'expert', split_axis=1, concat_axis=0, tiled=True)  22.1 us

commit v1 on v0

v1 whole, which is shorter than its diff:
```python
import functools

import jax
import jax.numpy as jnp
from jax import lax
from jax.experimental import pallas as pl
from jax.experimental.pallas import tpu as pltpu
from jax.sharding import PartitionSpec as P

epsilon = 1e-06
D = 1408
TOK = 256
E = 64
FH = 640
ROWS = 64
HALF = 32
COLS = D // 128
SLAB = 12
YS, ZS = 4, 16
F32, BF16 = jnp.float32, jnp.bfloat16
MESH = pl.DeviceIdType.MESH
OWN, LEFT, RIGHT, FAR = 0, 1, 2, 3


def to_slabs(value, wide, slabs):
    flat = wide.reshape(ROWS * 16, 128)
    for j in range(COLS):
        flat[pl.ds(j, ROWS, stride=16), :] = value[:, j * 128 : (j + 1) * 128]
    slabs[...] = wide[...][:, :SLAB, :].astype(BF16)


def from_slabs(slabs, wide, out):
    wide[:, :SLAB, :] = slabs[...].astype(F32)
    flat = wide.reshape(ROWS * 16, 128)
    for j in range(COLS):
        out[:, j * 128 : (j + 1) * 128] = flat[pl.ds(j, ROWS, stride=16), :].astype(BF16)


def far_first(i, y, z):
    m = i // 4
    odd = m % 2
    dz = (1 - 2 * odd) * (m // 2 - 8) - odd
    dy = 3 - i % 4
    return ((y + dy) % YS) * ZS + (z + dz + ZS) % ZS


def kernel(
    images, gain, slots, scale, up, down,
    back, comb,
    x_v, gain_v, slots_v, up_v, down_v, up_t, normed, wide,
    send_a, recv_a, send_d, recv_d,
    gat, hid, q_acc, p_out, p_in, q_out, r_far, r_fin,
    load_sem, a2a_sem, bs, br, cs, cr,
):
    sec, me = lax.axis_index("section"), lax.axis_index("expert")
    xs, core = sec // 2, sec % 2
    y, z = me // ZS, me % ZS
    partner = sec + 1 - 2 * core
    right = ((xs + 1) % 4) * 2 + core
    left = ((xs + 3) % 4) * 2 + core

    barrier = pltpu.get_barrier_semaphore()

    def greet(i, c):
        pl.semaphore_signal(barrier, inc=1, device_id={"expert": far_first(i, y, z)}, device_id_type=MESH)
        return c

    lax.fori_loop(0, E - 1, greet, 0)
    for peer in (left, right, partner):
        pl.semaphore_signal(barrier, inc=1, device_id={"section": peer}, device_id_type=MESH)

    loads = [
        pltpu.make_async_copy(src, dst, load_sem.at[i])
        for i, (src, dst) in enumerate(
            ((images.at[0], x_v), (gain, gain_v), (slots, slots_v), (up.at[0], up_v), (down.at[0], down_v))
        )
    ]
    for c in loads:
        c.start()
    for c in loads[:3]:
        c.wait()

    x = x_v[...].astype(F32)
    spread = jnp.mean(x * x, axis=-1, keepdims=True)
    normed[...] = (x * lax.rsqrt(spread + epsilon) * gain_v[...].astype(F32)).astype(BF16)
    n32 = normed[...].astype(F32)
    token_norm = jnp.sqrt(jnp.sum(n32 * n32, axis=-1, keepdims=True) + epsilon)
    cols = slots_v[...].astype(F32)
    column_norm = jnp.sqrt(jnp.sum(cols * cols, axis=0, keepdims=True) + epsilon)
    raw = jnp.dot(normed[...], slots_v[...], preferred_element_type=F32)
    scores = jnp.exp(scale[0] * raw / (token_norm * column_norm))
    dispatch = (scores / jnp.sum(scores, axis=0, keepdims=True)).astype(BF16)
    comb[...] = (scores / jnp.sum(scores, axis=1, keepdims=True)).astype(BF16)
    slot_in = lax.dot_general(dispatch, normed[...], (((0,), (0,)), ((), ())), preferred_element_type=F32)
    to_slabs(slot_in, wide, send_a)

    pl.semaphore_wait(barrier, E - 1 + 3)

    def scatter(src, dst, s, r):
        def one(i, c):
            there = far_first(i, y, z)
            pltpu.make_async_remote_copy(
                src.at[there], dst.at[me], a2a_sem.at[s], a2a_sem.at[r], device_id={"expert": there}, device_id_type=MESH
            ).start()
            return c

        lax.fori_loop(0, E - 1, one, 0)
        dst[me] = src[me]

    def all_but_one(buf, s):
        pltpu.make_async_copy(buf.at[pl.ds(0, E - 1)], buf.at[pl.ds(0, E - 1)], a2a_sem.at[s]).wait()

    scatter(send_a, recv_a, 0, 1)
    for c in loads[3:]:
        c.wait()
    for i in range(FH // 128):
        up_t[:, i * 128 : (i + 1) * 128] = up_v[i * 128 : (i + 1) * 128, :].T
    all_but_one(recv_a, 1)
    from_slabs(recv_a, wide, gat.at[OWN, pl.ds(0, ROWS)])

    def rows(group, half, other=0):
        return gat.at[group, pl.ds(other * ROWS + half * HALF, HALF)]

    def section_copy(src, dst, s, r, i, peer):
        return pltpu.make_async_remote_copy(src, dst, s.at[i], r.at[i], device_id={"section": peer}, device_id_type=MESH)

    hops = [
        section_copy(rows(OWN, 0), rows(LEFT, 0), bs, br, 0, right),
        section_copy(rows(OWN, 1), rows(RIGHT, 1), bs, br, 1, left),
        section_copy(rows(OWN, 1), rows(LEFT, 1), bs, br, 2, right),
        section_copy(rows(OWN, 0), rows(RIGHT, 0), bs, br, 3, left),
        section_copy(gat.at[OWN, pl.ds(0, ROWS)], gat.at[OWN, pl.ds(ROWS, ROWS)], bs, br, 4, partner),
        section_copy(rows(LEFT, 0), rows(FAR, 0), bs, br, 5, right),
        section_copy(rows(RIGHT, 1), rows(FAR, 1), bs, br, 6, left),
    ]
    across = {
        (g, h): section_copy(rows(g, h), rows(g, h, 1), bs, br, 5 + 2 * g + h, partner) for g in (1, 2, 3) for h in (0, 1)
    }

    def mlp(group):
        up_out = jnp.dot(gat[group], up_t[...], preferred_element_type=F32)
        hid[...] = jax.nn.gelu(up_out).astype(BF16)
        part = jnp.dot(hid[...], down_v[...], preferred_element_type=F32)
        q_acc[group] = part[:ROWS]
        p_out[group] = part[ROWS:].astype(BF16)

    pair = [section_copy(p_out.at[g], p_in.at[g], cs, cr, g, partner) for g in range(4)]

    def half(ref, h):
        return ref.at[pl.ds(h * HALF, HALF)]

    sums = [
        section_copy(half(q_out.at[FAR], 0), half(r_far, 0), cs, cr, 4, right),
        section_copy(half(q_out.at[FAR], 1), half(r_far, 1), cs, cr, 5, left),
        section_copy(half(q_out.at[RIGHT], 1), half(r_fin.at[0], 1), cs, cr, 6, right),
        section_copy(half(q_out.at[LEFT], 0), half(r_fin.at[1], 0), cs, cr, 7, left),
        section_copy(half(q_out.at[RIGHT], 0), half(r_fin.at[0], 0), cs, cr, 8, right),
        section_copy(half(q_out.at[LEFT], 1), half(r_fin.at[1], 1), cs, cr, 9, left),
    ]

    def chip_sum(group):
        pair[group].wait_recv()
        q_acc[group] = q_acc[group] + p_in[group].astype(F32)

    for c in hops[:5]:
        c.start()
    hops[4].wait_recv()
    mlp(OWN)
    pair[OWN].start()
    hops[0].wait_recv()
    hops[5].start()
    across[LEFT, 0].start()
    hops[1].wait_recv()
    hops[6].start()
    across[RIGHT, 1].start()
    hops[2].wait_recv()
    across[LEFT, 1].start()
    hops[3].wait_recv()
    across[RIGHT, 0].start()
    chip_sum(OWN)
    for h in (0, 1):
        across[LEFT, h].wait_recv()
    mlp(LEFT)
    pair[LEFT].start()
    for h in (0, 1):
        across[RIGHT, h].wait_recv()
    mlp(RIGHT)
    pair[RIGHT].start()
    for h in (0, 1):
        hops[5 + h].wait_recv()
        across[FAR, h].start()
    chip_sum(LEFT)
    q_out[LEFT, pl.ds(0, HALF)] = q_acc[LEFT, pl.ds(0, HALF)].astype(BF16)
    sums[3].start()
    chip_sum(RIGHT)
    q_out[RIGHT, pl.ds(HALF, HALF)] = q_acc[RIGHT, pl.ds(HALF, HALF)].astype(BF16)
    sums[2].start()
    for h in (0, 1):
        across[FAR, h].wait_recv()
    mlp(FAR)
    pair[FAR].start()
    chip_sum(FAR)
    q_out[FAR] = q_acc[FAR].astype(BF16)
    sums[0].start()
    sums[1].start()
    sums[0].wait_recv()
    q_out[RIGHT, pl.ds(0, HALF)] = (q_acc[RIGHT, pl.ds(0, HALF)] + r_far[pl.ds(0, HALF)].astype(F32)).astype(BF16)
    sums[4].start()
    sums[1].wait_recv()
    q_out[LEFT, pl.ds(HALF, HALF)] = (q_acc[LEFT, pl.ds(HALF, HALF)] + r_far[pl.ds(HALF, HALF)].astype(F32)).astype(BF16)
    sums[5].start()
    for i in (2, 3, 4, 5):
        sums[i].wait_recv()
    result = q_acc[OWN] + r_fin[0].astype(F32) + r_fin[1].astype(F32)
    to_slabs(result, wide, send_d)

    scatter(send_d, recv_d, 2, 3)
    for c in hops + list(across.values()) + pair + sums:
        c.wait_send()
    all_but_one(send_a, 0)
    all_but_one(send_d, 2)
    all_but_one(recv_d, 3)
    from_slabs(recv_d, wide, back)


def exchange(images, norm_gain, slot_map, logit_scale, up_weight, down_weight):
    any_, vmem = pl.BlockSpec(memory_space=pl.ANY), pl.BlockSpec(memory_space=pltpu.VMEM)
    dma = pltpu.SemaphoreType.DMA
    return pl.pallas_call(
        kernel,
        out_shape=(jax.ShapeDtypeStruct((E, D), BF16), jax.ShapeDtypeStruct((TOK, E), BF16)),
        in_specs=[any_, any_, any_, pl.BlockSpec(memory_space=pltpu.SMEM), any_, any_],
        out_specs=(vmem, vmem),
        scratch_shapes=[
            pltpu.VMEM((TOK, D), BF16), pltpu.VMEM((1, D), BF16), pltpu.VMEM((D, E), BF16),
            pltpu.VMEM((FH, D), BF16), pltpu.VMEM((FH, D), BF16), pltpu.VMEM((D, FH), BF16),
            pltpu.VMEM((TOK, D), BF16), pltpu.VMEM((ROWS, 16, 128), F32),
            *[pltpu.VMEM((E, SLAB, 128), BF16)] * 4,
            pltpu.VMEM((4, 2 * ROWS, D), BF16), pltpu.VMEM((2 * ROWS, FH), BF16), pltpu.VMEM((4, ROWS, D), F32),
            pltpu.VMEM((4, ROWS, D), BF16), pltpu.VMEM((4, ROWS, D), BF16), pltpu.VMEM((4, ROWS, D), BF16),
            pltpu.VMEM((ROWS, D), BF16), pltpu.VMEM((2, ROWS, D), BF16),
            dma((5,)), dma((4,)), dma((13,)), dma((13,)), dma((10,)), dma((10,)),
        ],
        compiler_params=pltpu.CompilerParams(collective_id=0, has_side_effects=True, vmem_limit_bytes=56 * 1024 * 1024),
    )(images, norm_gain.reshape(1, D), slot_map, logit_scale, up_weight, down_weight)


def local(images, norm_gain, slot_map, logit_scale, up_weight, down_weight):
    back, comb = exchange(images, norm_gain, slot_map, logit_scale, up_weight, down_weight)
    mixed = jnp.einsum("te,ed->td", comb, back, preferred_element_type=F32)
    return (images.astype(F32) + mixed[None]).astype(BF16)


def solution(mesh):
    return jax.shard_map(
        local,
        mesh=mesh,
        in_specs=(
            P(("section", "expert"), None, None),
            P(),
            P(),
            P(),
            P("expert", "section", None),
            P("expert", "section", None),
        ),
        out_specs=P(("section", "expert"), None, None),
        check_vma=False,
    )
```

time: 141 us -> 75.5 us (0.54); the launches traced: 139 us -> 75.4 us
  blocking collectives: 123 us -> 0 us
  Pallas kernels: 0 us -> 69.4 us
  other arithmetic: 8.99 us -> 0 us
  matrix products: 4.96 us -> 2.14 us
    all_to_all x4 -> x0, blocking collectives: 123 us -> none  [the longest x1 38.7 us: summed_on_arrival(): parts = lax.all_to_all(cut_along(array, dim, peers), axis, 0, 0, tiled=True)]
    pallas_call x0 -> x1, Pallas kernels: none -> 69.4 us  [exchange(): pl.pallas_call(kernel, out_shape=(jax.ShapeDtypeStruct((E, D), BF16), jax...]
    reduce_sum x4 -> x0, other arithmetic: 5.89 us -> none  [the longest x1 1.96 us: summed_on_arrival(): return jnp.sum(parts, axis=0)]
    dot_general x5 -> x1, matrix products: 4.96 us -> 2.14 us  [local(): mixed = jnp.einsum('te,ed->td', comb, back, preferred_element_type=F32)]
    unnamed x1 -> x0, other arithmetic: 1.69 us -> none
where the time goes in v1:
time: 75.5 us; the launch traced here: 75.4 us
  Pallas kernels  69.4 us (92%)
  local copies, waits for them, and re-layouts  3.12 us (4%)
  matrix products  2.14 us (3%)
    pallas_call x1, Pallas kernels, exchange(): pl.pallas_call(kernel, out_shape=(jax.ShapeDtypeStruct((E, D), BF16), jax...  69.4 us
    dot_general x1, matrix products, local(): mixed = jnp.einsum('te,ed->td', comb, back, preferred_element_type=F32)  2.14 us
    unnamed x3, local copies, waits for them, and re-layouts  1.83 us

profile of v1, /device:TPU:1, one launch (start us, length us, event | category | flops | bytes accessed | tf_op | source)
XLA Modules:
  0.0 75.4 jit_solution(14185789866989960261)
XLA Ops:
  0.7 1.3 %reshape.3.gain = bf16[1,1408]{1,0:T(2,128)(2,1)} reshape(bf16[1408]{0:T(1024)(128)(2,1)} %param.7) | data formatting | bytes 5632 | tf_op jit(solution)/shard_map/reshape | solution.py:245
  1.9 1.8 %copy.7.slots = bf16[1408,64]{1,0:T(8,128)(2,1)} copy(bf16[1408,64]{0,1:T(8,128)(2,1)} %param.8) | data formatting | bytes 360448 | tf_op args[2]
  3.8 0.0 copy-start
  3.8 69.4 %shard_map.64 = (bf16[64,1408]{1,0:T(8,128)(2,1)}, bf16[256,64]{1,0:T(8,128)(2,1)}) custom-call(bf16[1,256,1408]{2,1,0:T(8,128)(2,1)} %images.1, bf16[1,1408]{1,0:T(2,128)(2,1)} %reshape.3.gain, bf16[1408,64]{1,0:T(8,128)(2,1)} %copy.7.slots, f32[1]{0:T(128)S(6)} %copy.8.scale, bf16[1,640,1408]{2,1,0:T(8,128)(2,1)} %up.1, bf16[1,640,1408]{2,1,0:T(8,128)(2,1)} %down.1), custom_call_target="tpu_custom_call" | custom-call | tf_op jit(solution)/shard_map/pallas_call | solution.py:229
  73.2 0.0 copy-done
  73.2 2.1 %fusion.1 = bf16[1,256,1408]{2,1,0:T(8,128)(2,1)} fusion(bf16[256,64]{1,0:T(8,128)(2,1)} %get-tuple-element.7, bf16[64,1408]{1,0:T(8,128)(2,1)} %get-tuple-element.8, bf16[1,256,1408]{2,1,0:T(8,128)(2,1)S(1)} %copy-done), kind=kOutput, calls=%fused_computation.2 | convolution fusion | flops 47218688 | bytes 1654784 | tf_op jit(solution)/shard_map/te,ed->td/dot_general | solution.py:250
Async XLA Ops:
  3.8 69.4 %copy-start = (bf16[1,256,1408]{2,1,0:T(8,128)(2,1)S(1)}, bf16[1,256,1408]{2,1,0:T(8,128)(2,1)}, u32[]{:S(2)}) copy-start(bf16[1,256,1408]{2,1,0:T(8,128)(2,1)} %images.1) | copy-start | bytes 2162692

commit v2 on v0

v2 whole, which is shorter than its diff:
```python
import jax
import jax.numpy as jnp
from jax import lax
from jax.experimental import pallas as pl
from jax.experimental.pallas import tpu as pltpu
from jax.sharding import PartitionSpec as P

epsilon = 1e-06
D = 1408
TOK = 256
E = 64
FH = 640
CH = 4
R = 16
COLS = D // 128
SLAB = 12
F32, BF16 = jnp.float32, jnp.bfloat16
MESH = pl.DeviceIdType.MESH
OWN, LEFT, RIGHT, FAR = 0, 1, 2, 3


def to_slabs(value, wide, slabs, n):
    flat = wide.reshape(n * 16, 128)
    for j in range(COLS):
        flat[pl.ds(j, n, stride=16), :] = value[:, j * 128 : (j + 1) * 128]
    slabs[...] = wide[...][:, :SLAB, :].astype(BF16)


def from_slabs(slabs, wide, out, n):
    wide[:, :SLAB, :] = slabs[...].astype(F32)
    flat = wide.reshape(n * 16, 128)
    for j in range(COLS):
        out[:, j * 128 : (j + 1) * 128] = flat[pl.ds(j, n, stride=16), :].astype(BF16)


def kernel(
    images, gain, slots, scale, up, down,
    back, comb,
    x_v, gain_v, slots_v, up_v, down_v, up_t, normed, wide, wide_in, wide_out,
    send_a, recv_a, send_d, recv_d,
    gat, hid, q_acc, p_out, p_in, q_out, r_far, r_fin,
    load_sem, a2a_s, a_r, d_r, bs, br, cs, cr,
):
    sec, me = lax.axis_index("section"), lax.axis_index("expert")
    xs, core = sec // 2, sec % 2
    y, z = me // 16, me % 16
    partner = sec + 1 - 2 * core
    right = ((xs + 1) % 4) * 2 + core
    left = ((xs + 3) % 4) * 2 + core
    by_dy = [((y + dy) % 4) * 16 for dy in (3, 2, 1, 0)]
    by_minus_dy = [((y + 4 - dy) % 4) * 16 for dy in (3, 2, 1, 0)]

    def dz_of(m):
        odd = m % 2
        return (1 - 2 * odd) * (m // 2 - 8) - odd + 16

    loads = [
        pltpu.make_async_copy(src, dst, load_sem.at[i])
        for i, (src, dst) in enumerate(
            ((slots, slots_v), (gain, gain_v), (images.at[0], x_v), (up.at[0], up_v), (down.at[0], down_v))
        )
    ]
    for c in loads:
        c.start()

    barrier = pltpu.get_barrier_semaphore()

    def greet(e):
        pl.semaphore_signal(barrier, inc=1, device_id={"expert": e}, device_id_type=MESH)

    def greet4(m, c):
        there = (z + dz_of(m)) % 16
        for base in by_dy:
            greet(base + there)
        return c

    lax.fori_loop(0, 15, greet4, 0)
    for base in by_dy[:3]:
        greet(base + z)
    for peer in (left, right, partner):
        pl.semaphore_signal(barrier, inc=1, device_id={"section": peer}, device_id_type=MESH)

    for c in loads[:3]:
        c.wait()
    x = x_v[...].astype(F32)
    spread = jnp.mean(x * x, axis=-1, keepdims=True)
    normed[...] = (x * lax.rsqrt(spread + epsilon) * gain_v[...].astype(F32).reshape(1, D)).astype(BF16)
    n32 = normed[...].astype(F32)
    token_norm = jnp.sqrt(jnp.sum(n32 * n32, axis=-1, keepdims=True) + epsilon)
    slot_cols = slots_v[...].T
    cols = slot_cols.astype(F32)
    column_norm = jnp.sqrt(jnp.sum(cols * cols, axis=0, keepdims=True) + epsilon)
    raw = jnp.dot(normed[...], slot_cols, preferred_element_type=F32)
    scores = jnp.exp(scale[0] * raw / (token_norm * column_norm))
    dispatch = (scores / jnp.sum(scores, axis=0, keepdims=True)).astype(BF16)
    comb[...] = (scores / jnp.sum(scores, axis=1, keepdims=True)).astype(BF16)
    slot_in = lax.dot_general(dispatch, normed[...], (((0,), (0,)), ((), ())), preferred_element_type=F32)
    to_slabs(slot_in, wide, send_a, E)

    pl.semaphore_wait(barrier, E - 1 + 3)

    def send_row(chunk, m, k, base, there):
        e = base + there
        i = m * 4 + k
        pltpu.make_async_remote_copy(
            send_a.at[e], recv_a.at[i], a2a_s.at[0], a_r.at[chunk], device_id={"expert": e}, device_id_type=MESH
        ).start()

    for chunk in range(CH):

        def send4(m, c, chunk=chunk):
            there = (z + dz_of(m)) % 16
            for k, base in enumerate(by_dy):
                send_row(chunk, m, k, base, there)
            return c

        lax.fori_loop(4 * chunk, min(4 * chunk + 4, 15), send4, 0)
    for k in range(3):
        send_row(CH - 1, 15, k, by_dy[k], z)
    recv_a[E - 1] = send_a[me]
    for c in loads[3:]:
        c.wait()
    for i in range(FH // 128):
        up_t[:, i * 128 : (i + 1) * 128] = up_v[i * 128 : (i + 1) * 128, :].T

    def slabs_in(buf, n, sem):
        pltpu.make_async_copy(buf.at[pl.ds(0, n)], buf.at[pl.ds(0, n)], sem).wait()

    def section_copy(src, dst, s, r, peer):
        return pltpu.make_async_remote_copy(src, dst, s, r, device_id={"section": peer}, device_id_type=MESH)

    def rows(k, group, n=1, other=0):
        return gat.at[k, pl.ds(64 * other + R * group, R * n)]

    def b_copy(k, i, src, dst, peer):
        return section_copy(src, dst, bs.at[k, i], br.at[k, i], peer)

    def c_copy(k, i, src, dst, peer):
        return section_copy(src, dst, cs.at[k, i], cr.at[k, i], peer)

    to_right, to_left, to_other, far_on, pair_on, far_other = [], [], [], [], [], []
    pair, c_one, c_far, c_two = [], [], [], []
    for k in range(CH):
        to_right.append(b_copy(k, 0, rows(k, OWN), rows(k, LEFT), right))
        to_left.append(b_copy(k, 1, rows(k, OWN), rows(k, RIGHT), left))
        to_other.append(b_copy(k, 2, rows(k, OWN), rows(k, OWN, 1, 1), partner))
        via, onward, near = (LEFT, right, left) if k % 2 == 0 else (RIGHT, left, right)
        far_on.append(b_copy(k, 3, rows(k, via), rows(k, FAR), onward))
        pair_on.append(b_copy(k, 4, rows(k, LEFT, 2), rows(k, LEFT, 2, 1), partner))
        far_other.append(b_copy(k, 5, rows(k, FAR), rows(k, FAR, 1, 1), partner))
        ahead, behind = (RIGHT, LEFT) if k % 2 == 0 else (LEFT, RIGHT)
        pair.append(c_copy(k, 0, p_out.at[k], p_in.at[k], partner))
        c_one.append(c_copy(k, 1, q_out.at[k, pl.ds(R * behind, R)], r_fin.at[k, 0], near))
        c_far.append(c_copy(k, 2, q_out.at[k, pl.ds(R * FAR, R)], r_far.at[k], onward))
        c_two.append(c_copy(k, 3, q_out.at[k, pl.ds(R * ahead, R)], r_fin.at[k, 1], onward))

    def s0(k):
        slabs_in(recv_a, R if k < CH - 1 else R - 1, a_r.at[k])
        from_slabs(recv_a.at[pl.ds(R * k, R)], wide_in.at[k], gat.at[k, pl.ds(0, R)], R)
        first, second = (to_right, to_left) if k % 2 == 0 else (to_left, to_right)
        first[k].start()
        second[k].start()
        to_other[k].start()

    def s1(k):
        first, second = (to_right, to_left) if k % 2 == 0 else (to_left, to_right)
        first[k].wait_recv()
        far_on[k].start()
        second[k].wait_recv()
        pair_on[k].start()

    def s2(k):
        far_on[k].wait_recv()
        far_other[k].start()

    def s3(k):
        to_other[k].wait_recv()
        pair_on[k].wait_recv()
        far_other[k].wait_recv()
        up_out = jnp.dot(gat[k], up_t[...], preferred_element_type=F32)
        hid[k] = jax.nn.gelu(up_out).astype(BF16)
        part = jnp.dot(hid[k], down_v[...], preferred_element_type=F32)
        p_out[k] = part[4 * R :].astype(BF16)
        pair[k].start()
        q_acc[k] = part[: 4 * R]

    def s4(k):
        pair[k].wait_recv()
        ahead, behind = (RIGHT, LEFT) if k % 2 == 0 else (LEFT, RIGHT)

        def summed(g):
            return q_acc[k, pl.ds(R * g, R)] + p_in[k, pl.ds(R * g, R)].astype(F32)

        q_out[k, pl.ds(R * FAR, R)] = summed(FAR).astype(BF16)
        c_far[k].start()
        q_out[k, pl.ds(R * behind, R)] = summed(behind).astype(BF16)
        c_one[k].start()
        for g in (ahead, OWN):
            q_acc[k, pl.ds(R * g, R)] = summed(g)

    def s5(k):
        c_far[k].wait_recv()
        g = RIGHT if k % 2 == 0 else LEFT
        q_out[k, pl.ds(R * g, R)] = (q_acc[k, pl.ds(R * g, R)] + r_far[k].astype(F32)).astype(BF16)
        c_two[k].start()

    def s6(k):
        c_one[k].wait_recv()
        c_two[k].wait_recv()
        result = q_acc[k, pl.ds(0, R)] + r_fin[k, 0].astype(F32) + r_fin[k, 1].astype(F32)
        to_slabs(result, wide_out.at[k], send_d.at[pl.ds(R * k, R)], R)

        def return_row(m, n, base, there):
            e = base + there
            pltpu.make_async_remote_copy(
                send_d.at[m * 4 + n], recv_d.at[me], a2a_s.at[1], d_r.at[0], device_id={"expert": e}, device_id_type=MESH
            ).start()

        def return4(m, c):
            there = (z + 32 - dz_of(m)) % 16
            for n, base in enumerate(by_minus_dy):
                return_row(m, n, base, there)
            return c

        lax.fori_loop(4 * k, min(4 * k + 4, 15), return4, 0)
        if k == CH - 1:
            for n in range(3):
                return_row(15, n, by_minus_dy[n], z)
            recv_d[me] = send_d[E - 1]

    stages = (s0, s1, s2, s3, s4, s5, s6)
    order = "00 10 01 02 20 03 11 30 12 21 40 13 31 22 50 32 41 23 33 42 60 51 43 52 61 53 62 63"
    for step in order.split():
        stages[int(step[0])](int(step[1]))

    for c in to_right + to_left + to_other + far_on + pair_on + far_other + pair + c_one + c_far + c_two:
        c.wait_send()
    slabs_in(send_a, E - 1, a2a_s.at[0])
    slabs_in(send_d, E - 1, a2a_s.at[1])
    slabs_in(recv_d, E - 1, d_r.at[0])
    from_slabs(recv_d, wide, back, E)


def exchange(images, norm_gain, slot_map, logit_scale, up_weight, down_weight):
    any_, vmem = pl.BlockSpec(memory_space=pl.ANY), pl.BlockSpec(memory_space=pltpu.VMEM)
    dma = pltpu.SemaphoreType.DMA
    return pl.pallas_call(
        kernel,
        out_shape=(jax.ShapeDtypeStruct((E, D), BF16), jax.ShapeDtypeStruct((TOK, E), BF16)),
        in_specs=[any_, any_, any_, pl.BlockSpec(memory_space=pltpu.SMEM), any_, any_],
        out_specs=(vmem, vmem),
        scratch_shapes=[
            pltpu.VMEM((TOK, D), BF16), pltpu.VMEM((D,), BF16), pltpu.VMEM((E, D), BF16),
            pltpu.VMEM((FH, D), BF16), pltpu.VMEM((FH, D), BF16), pltpu.VMEM((D, FH), BF16),
            pltpu.VMEM((TOK, D), BF16), pltpu.VMEM((E, 16, 128), F32),
            pltpu.VMEM((CH, R, 16, 128), F32), pltpu.VMEM((CH, R, 16, 128), F32),
            *[pltpu.VMEM((E, SLAB, 128), BF16)] * 4,
            pltpu.VMEM((CH, 8 * R, D), BF16), pltpu.VMEM((CH, 8 * R, FH), BF16), pltpu.VMEM((CH, 4 * R, D), F32),
            pltpu.VMEM((CH, 4 * R, D), BF16), pltpu.VMEM((CH, 4 * R, D), BF16), pltpu.VMEM((CH, 4 * R, D), BF16),
            pltpu.VMEM((CH, R, D), BF16), pltpu.VMEM((CH, 2, R, D), BF16),
            dma((5,)), dma((2,)), dma((CH,)), dma((1,)), dma((CH, 6)), dma((CH, 6)), dma((CH, 4)), dma((CH, 4)),
        ],
        compiler_params=pltpu.CompilerParams(collective_id=0, has_side_effects=True, vmem_limit_bytes=56 * 1024 * 1024),
    )(images, norm_gain, slot_map.T, logit_scale, up_weight, down_weight)


def local(images, norm_gain, slot_map, logit_scale, up_weight, down_weight):
    back, comb = exchange(images, norm_gain, slot_map, logit_scale, up_weight, down_weight)
    mixed = jnp.einsum("te,ed->td", comb, back, preferred_element_type=F32)
    return (images.astype(F32) + mixed[None]).astype(BF16)


def solution(mesh):
    return jax.shard_map(
        local,
        mesh=mesh,
        in_specs=(
            P(("section", "expert"), None, None),
            P(),
            P(),
            P(),
            P("expert", "section", None),
            P("expert", "section", None),
        ),
        out_specs=P(("section", "expert"), None, None),
        check_vma=False,
    )
```

time: 141 us -> 67.8 us (0.48); the launches traced: 139 us -> 67.7 us
  blocking collectives: 123 us -> 0 us
  Pallas kernels: 0 us -> 64.8 us
  other arithmetic: 8.99 us -> 0 us
  matrix products: 4.96 us -> 2.14 us
  local copies, waits for them, and re-layouts: 1.82 us -> 0.01 us
    all_to_all x4 -> x0, blocking collectives: 123 us -> none  [the longest x1 38.7 us: summed_on_arrival(): parts = lax.all_to_all(cut_along(array, dim, peers), axis, 0, 0, tiled=True)]
    pallas_call x0 -> x1, Pallas kernels: none -> 64.8 us  [exchange(): pl.pallas_call(kernel, out_shape=(jax.ShapeDtypeStruct((E, D), BF16), jax...]
    reduce_sum x4 -> x0, other arithmetic: 5.89 us -> none  [the longest x1 1.96 us: summed_on_arrival(): return jnp.sum(parts, axis=0)]
    dot_general x5 -> x1, matrix products: 4.96 us -> 2.14 us  [local(): mixed = jnp.einsum('te,ed->td', comb, back, preferred_element_type=F32)]
    unnamed x1 -> x0, other arithmetic: 1.69 us -> none
where the time goes in v2:
time: 67.8 us; the launch traced here: 67.7 us
  Pallas kernels  64.8 us (96%)
  matrix products  2.14 us (3%)
  between operations  0.68 us (1%)
    pallas_call x1, Pallas kernels, exchange(): pl.pallas_call(kernel, out_shape=(jax.ShapeDtypeStruct((E, D), BF16), jax...  64.8 us
    dot_general x1, matrix products, local(): mixed = jnp.einsum('te,ed->td', comb, back, preferred_element_type=F32)  2.14 us

profile of v2, /device:TPU:1, one launch (start us, length us, event | category | flops | bytes accessed | tf_op | source)
XLA Modules:
  0.0 67.7 jit_solution(10086316218204729890)
XLA Ops:
  0.7 0.0 copy-start
  0.7 64.8 %shard_map.64 = (bf16[64,1408]{1,0:T(8,128)(2,1)}, bf16[256,64]{1,0:T(8,128)(2,1)}) custom-call(bf16[1,256,1408]{2,1,0:T(8,128)(2,1)} %images.1, bf16[1408]{0:T(1024)(128)(2,1)} %gain.1, bf16[64,1408]{1,0:T(8,128)(2,1)} %bitcast.9, f32[1]{0:T(128)S(6)} %copy.7.scale, bf16[1,640,1408]{2,1,0:T(8,128)(2,1)} %up.1, bf16[1,640,1408]{2,1,0:T(8,128)(2,1)} %down.1), custom_call_target="tpu_custom_call" | custom-call | tf_op jit(solution)/shard_map/pallas_call | solution.py:247
  65.5 0.0 copy-done
  65.5 2.1 %fusion.1 = bf16[1,256,1408]{2,1,0:T(8,128)(2,1)} fusion(bf16[256,64]{1,0:T(8,128)(2,1)} %get-tuple-element.7, bf16[64,1408]{1,0:T(8,128)(2,1)} %get-tuple-element.8, bf16[1,256,1408]{2,1,0:T(8,128)(2,1)S(1)} %copy-done), kind=kOutput, calls=%fused_computation.2 | convolution fusion | flops 47218688 | bytes 1654784 | tf_op jit(solution)/shard_map/te,ed->td/dot_general | solution.py:269
Async XLA Ops:
  0.7 64.9 %copy-start = (bf16[1,256,1408]{2,1,0:T(8,128)(2,1)S(1)}, bf16[1,256,1408]{2,1,0:T(8,128)(2,1)}, u32[]{:S(2)}) copy-start(bf16[1,256,1408]{2,1,0:T(8,128)(2,1)} %images.1) | copy-start | bytes 2162692

commit v3 on v2

v3 whole, which is shorter than its diff:
```python
import jax
import jax.numpy as jnp
from jax import lax
from jax.experimental import pallas as pl
from jax.experimental.pallas import tpu as pltpu
from jax.sharding import PartitionSpec as P

epsilon = 1e-06
D = 1408
TOK = 256
E = 64
FH = 640
CH = 4
GROUPS = 4
R = E // CH
GPC = GROUPS // CH
COLS = D // 128
SLAB = 12
F32, BF16 = jnp.float32, jnp.bfloat16
MESH = pl.DeviceIdType.MESH
OWN, LEFT, RIGHT, FAR = 0, 1, 2, 3


def to_slabs(value, wide, slabs, n):
    flat = wide.reshape(n * 16, 128)
    for j in range(COLS):
        flat[pl.ds(j, n, stride=16), :] = value[:, j * 128 : (j + 1) * 128]
    slabs[...] = wide[...][:, :SLAB, :].astype(BF16)


def from_slabs(slabs, wide, out, n):
    wide[:, :SLAB, :] = slabs[...].astype(F32)
    flat = wide.reshape(n * 16, 128)
    for j in range(COLS):
        out[:, j * 128 : (j + 1) * 128] = flat[pl.ds(j, n, stride=16), :].astype(BF16)


def kernel(
    images, gain, slots, scale, up, down,
    back, comb,
    x_v, gain_v, slots_v, up_v, down_v, up_t, normed, wide, wide_in, wide_out,
    send_a, recv_a, send_d, recv_d,
    gat, hid, q_acc, p_out, p_in, q_out, r_fin,
    load_sem, a2a_s, a_r, d_r, bs, br, cs, cr,
):
    sec, me = lax.axis_index("section"), lax.axis_index("expert")
    xs, core = sec // 2, sec % 2
    y, z = me // 16, me % 16
    partner = sec + 1 - 2 * core
    right = ((xs + 1) % 4) * 2 + core
    left = ((xs + 3) % 4) * 2 + core
    far = ((xs + 2) % 4) * 2 + core
    by_dy = [((y + dy) % 4) * 16 for dy in (3, 2, 1, 0)]
    by_minus_dy = [((y + 4 - dy) % 4) * 16 for dy in (3, 2, 1, 0)]

    def dz_of(k, j):
        odd = j % 2
        return (1 - 2 * odd) * (8 - k + (j // 2) * (2 * k - 7)) + odd + 16

    def each_row(k, do):
        def four(j, c):
            for n in range(4):
                do(16 * k + 4 * j + n, n, dz_of(k, j))
            return c

        lax.fori_loop(0, 3 if k == 0 else 4, four, 0)
        if k == 0:
            for n in range(3):
                do(12 + n, n, 16)

    loads = [
        pltpu.make_async_copy(src, dst, load_sem.at[i])
        for i, (src, dst) in enumerate(
            ((slots, slots_v), (gain, gain_v), (images.at[0], x_v), (up.at[0], up_v), (down.at[0], down_v))
        )
    ]
    for c in loads:
        c.start()

    barrier = pltpu.get_barrier_semaphore()

    def greet(e):
        pl.semaphore_signal(barrier, inc=1, device_id={"expert": e}, device_id_type=MESH)

    for g in range(GROUPS):
        each_row(g, lambda i, n, dz: greet(by_dy[n] + (z + dz) % 16))
    for peer in (left, right, far, partner):
        pl.semaphore_signal(barrier, inc=1, device_id={"section": peer}, device_id_type=MESH)

    for c in loads[:3]:
        c.wait()
    x = x_v[...].astype(F32)
    spread = jnp.mean(x * x, axis=-1, keepdims=True)
    normed[...] = (x * lax.rsqrt(spread + epsilon) * gain_v[...].astype(F32).reshape(1, D)).astype(BF16)
    n32 = normed[...].astype(F32)
    token_norm = jnp.sqrt(jnp.sum(n32 * n32, axis=-1, keepdims=True) + epsilon)
    slot_cols = slots_v[...].T
    cols = slot_cols.astype(F32)
    column_norm = jnp.sqrt(jnp.sum(cols * cols, axis=0, keepdims=True) + epsilon)
    raw = jnp.dot(normed[...], slot_cols, preferred_element_type=F32)
    scores = jnp.exp(scale[0] * raw / (token_norm * column_norm))
    dispatch = (scores / jnp.sum(scores, axis=0, keepdims=True)).astype(BF16)
    comb[...] = (scores / jnp.sum(scores, axis=1, keepdims=True)).astype(BF16)
    slot_in = lax.dot_general(dispatch, normed[...], (((0,), (0,)), ((), ())), preferred_element_type=F32)
    to_slabs(slot_in, wide, send_a, E)

    pl.semaphore_wait(barrier, E - 1 + 4)

    def send_row(k, i, e):
        pltpu.make_async_remote_copy(
            send_a.at[e], recv_a.at[i], a2a_s.at[0], a_r.at[k], device_id={"expert": e}, device_id_type=MESH
        ).start()

    for g in range(GROUPS):
        each_row(g, lambda i, n, dz, g=g: send_row(g // GPC, i, by_dy[n] + (z + dz) % 16))
    recv_a[15] = send_a[me]
    for c in loads[3:]:
        c.wait()
    for i in range(FH // 128):
        up_t[:, i * 128 : (i + 1) * 128] = up_v[i * 128 : (i + 1) * 128, :].T

    def slabs_in(buf, n, sem):
        pltpu.make_async_copy(buf.at[pl.ds(0, n)], buf.at[pl.ds(0, n)], sem).wait()

    def section_copy(src, dst, s, r, peer):
        return pltpu.make_async_remote_copy(src, dst, s, r, device_id={"section": peer}, device_id_type=MESH)

    def rows(k, group, n=1, other=0):
        return gat.at[k, pl.ds(4 * R * other + R * group, R * n)]

    def b_copy(k, i, src, dst, peer):
        return section_copy(src, dst, bs.at[k, i], br.at[k, i], peer)

    def c_copy(k, i, group, slot, peer):
        return section_copy(q_out.at[k, pl.ds(R * group, R)], r_fin.at[k, slot], cs.at[k, i], cr.at[k, i], peer)

    hops, to_other, on, pair, sums = ([] for _ in range(5))
    for k in range(CH):
        hops.append([
            b_copy(k, 0, rows(k, OWN), rows(k, FAR), far),
            b_copy(k, 1, rows(k, OWN), rows(k, LEFT), right),
            b_copy(k, 2, rows(k, OWN), rows(k, RIGHT), left),
        ])
        to_other.append(b_copy(k, 3, rows(k, OWN), rows(k, OWN, 1, 1), partner))
        on.append(b_copy(k, 4, rows(k, LEFT, 3), rows(k, LEFT, 3, 1), partner))
        pair.append(section_copy(p_out.at[k], p_in.at[k], cs.at[k, 0], cr.at[k, 0], partner))
        sums.append([c_copy(k, 1, FAR, 2, far), c_copy(k, 2, LEFT, 0, left), c_copy(k, 3, RIGHT, 1, right)])

    def s0(k):
        slabs_in(recv_a, R if k else R - 1, a_r.at[k])
        from_slabs(recv_a.at[pl.ds(R * k, R)], wide_in.at[k], gat.at[k, pl.ds(0, R)], R)
        for c in hops[k]:
            c.start()
        to_other[k].start()

    def s1(k):
        for c in hops[k]:
            c.wait_recv()
        on[k].start()

    def s2(k):
        to_other[k].wait_recv()
        on[k].wait_recv()
        up_out = jnp.dot(gat[k], up_t[...], preferred_element_type=F32)
        hid[k] = jax.nn.gelu(up_out).astype(BF16)
        part = jnp.dot(hid[k], down_v[...], preferred_element_type=F32)
        p_out[k] = part[4 * R :].astype(BF16)
        pair[k].start()
        q_acc[k] = part[: 4 * R]

    def s3(k):
        pair[k].wait_recv()
        for group, c in zip((FAR, LEFT, RIGHT), sums[k]):
            at = pl.ds(R * group, R)
            q_out[k, at] = (q_acc[k, at] + p_in[k, at].astype(F32)).astype(BF16)
            c.start()
        q_acc[k, pl.ds(0, R)] = q_acc[k, pl.ds(0, R)] + p_in[k, pl.ds(0, R)].astype(F32)

    def s4(k):
        for c in sums[k]:
            c.wait_recv()
        r0, r1, r2 = (r_fin[k, n].astype(F32) for n in range(3))
        result = (q_acc[k, pl.ds(0, R)] + r0) + (r1 + r2)
        to_slabs(result, wide_out.at[k], send_d.at[pl.ds(R * k, R)], R)

        def return_row(i, e):
            pltpu.make_async_remote_copy(
                send_d.at[i], recv_d.at[me], a2a_s.at[1], d_r.at[0], device_id={"expert": e}, device_id_type=MESH
            ).start()

        for g in range(GPC * k, GPC * (k + 1)):
            each_row(g, lambda i, n, dz: return_row(i, by_minus_dy[n] + (z + 32 - dz) % 16))
        if k == 0:
            recv_d[me] = send_d[15]

    stages = (s0, s1, s2, s3, s4)
    order = (0, 1, 10, 2, 20, 11, 3, 30, 21, 12, 31, 22, 13, 40, 32, 23, 41, 33, 42, 43)
    for step in order:
        stages[step // 10](step % 10)

    for c in to_other + on + pair + sum(hops + sums, []):
        c.wait_send()
    slabs_in(send_a, E - 1, a2a_s.at[0])
    slabs_in(send_d, E - 1, a2a_s.at[1])
    slabs_in(recv_d, E - 1, d_r.at[0])
    from_slabs(recv_d, wide, back, E)


def exchange(images, norm_gain, slot_map, logit_scale, up_weight, down_weight):
    hbm, vmem = pl.BlockSpec(memory_space=pl.ANY), pl.BlockSpec(memory_space=pltpu.VMEM)
    dma = pltpu.SemaphoreType.DMA
    return pl.pallas_call(
        kernel,
        out_shape=(jax.ShapeDtypeStruct((E, D), BF16), jax.ShapeDtypeStruct((TOK, E), BF16)),
        in_specs=[hbm, hbm, hbm, pl.BlockSpec(memory_space=pltpu.SMEM), hbm, hbm],
        out_specs=(vmem, vmem),
        scratch_shapes=[
            pltpu.VMEM((TOK, D), BF16), pltpu.VMEM((D,), BF16), pltpu.VMEM((E, D), BF16),
            pltpu.VMEM((FH, D), BF16), pltpu.VMEM((FH, D), BF16), pltpu.VMEM((D, FH), BF16),
            pltpu.VMEM((TOK, D), BF16), pltpu.VMEM((E, 16, 128), F32),
            pltpu.VMEM((CH, R, 16, 128), F32), pltpu.VMEM((CH, R, 16, 128), F32),
            *[pltpu.VMEM((E, SLAB, 128), BF16)] * 4,
            pltpu.VMEM((CH, 8 * R, D), BF16), pltpu.VMEM((CH, 8 * R, FH), BF16), pltpu.VMEM((CH, 4 * R, D), F32),
            pltpu.VMEM((CH, 4 * R, D), BF16), pltpu.VMEM((CH, 4 * R, D), BF16), pltpu.VMEM((CH, 4 * R, D), BF16),
            pltpu.VMEM((CH, 3, R, D), BF16),
            dma((5,)), dma((2,)), dma((CH,)), dma((1,)), dma((CH, 5)), dma((CH, 5)), dma((CH, 4)), dma((CH, 4)),
        ],
        compiler_params=pltpu.CompilerParams(collective_id=0, has_side_effects=True, vmem_limit_bytes=56 * 1024 * 1024),
    )(images, norm_gain, slot_map.T, logit_scale, up_weight, down_weight)


def local(images, norm_gain, slot_map, logit_scale, up_weight, down_weight):
    back, comb = exchange(images, norm_gain, slot_map, logit_scale, up_weight, down_weight)
    mixed = jnp.einsum("te,ed->td", comb, back, preferred_element_type=F32)
    return (images.astype(F32) + mixed[None]).astype(BF16)


def solution(mesh):
    return jax.shard_map(
        local,
        mesh=mesh,
        in_specs=(
            P(("section", "expert"), None, None),
            P(),
            P(),
            P(),
            P("expert", "section", None),
            P("expert", "section", None),
        ),
        out_specs=P(("section", "expert"), None, None),
        check_vma=False,
    )
```

time: 67.8 us -> 61.1 us (0.901)
  Pallas kernels: 64.8 us -> 58.2 us
    pallas_call x1, Pallas kernels: 64.8 us -> 58.2 us  [exchange(): pl.pallas_call(kernel, out_shape=(jax.ShapeDtypeStruct((E, D), BF16), jax...]
where the time goes in v3:
time: 61.1 us; the launch traced here: 61 us
  Pallas kernels  58.2 us (95%)
  matrix products  2.15 us (4%)
  between operations  0.68 us (1%)
    pallas_call x1, Pallas kernels, exchange(): pl.pallas_call(kernel, out_shape=(jax.ShapeDtypeStruct((E, D), BF16), jax...  58.2 us
    dot_general x1, matrix products, local(): mixed = jnp.einsum('te,ed->td', comb, back, preferred_element_type=F32)  2.15 us

profile of v3, /device:TPU:1, one launch (start us, length us, event | category | flops | bytes accessed | tf_op | source)
XLA Modules:
  0.0 61.0 jit_solution(15306934877445324918)
XLA Ops:
  0.7 0.0 copy-start
  0.7 58.2 %shard_map.64 = (bf16[64,1408]{1,0:T(8,128)(2,1)}, bf16[256,64]{1,0:T(8,128)(2,1)}) custom-call(bf16[1,256,1408]{2,1,0:T(8,128)(2,1)} %images.1, bf16[1408]{0:T(1024)(128)(2,1)} %gain.1, bf16[64,1408]{1,0:T(8,128)(2,1)} %bitcast.9, f32[1]{0:T(128)S(6)} %copy.7.scale, bf16[1,640,1408]{2,1,0:T(8,128)(2,1)} %up.1, bf16[1,640,1408]{2,1,0:T(8,128)(2,1)} %down.1), custom_call_target="tpu_custom_call" | custom-call | tf_op jit(solution)/shard_map/pallas_call | solution.py:212
  58.8 0.0 copy-done
  58.9 2.1 %fusion.1 = bf16[1,256,1408]{2,1,0:T(8,128)(2,1)} fusion(bf16[256,64]{1,0:T(8,128)(2,1)} %get-tuple-element.7, bf16[64,1408]{1,0:T(8,128)(2,1)} %get-tuple-element.8, bf16[1,256,1408]{2,1,0:T(8,128)(2,1)S(1)} %copy-done), kind=kOutput, calls=%fused_computation.2 | convolution fusion | flops 47218688 | bytes 1654784 | tf_op jit(solution)/shard_map/te,ed->td/dot_general | solution.py:234
Async XLA Ops:
  0.7 58.2 %copy-start = (bf16[1,256,1408]{2,1,0:T(8,128)(2,1)S(1)}, bf16[1,256,1408]{2,1,0:T(8,128)(2,1)}, u32[]{:S(2)}) copy-start(bf16[1,256,1408]{2,1,0:T(8,128)(2,1)} %images.1) | copy-start | bytes 2162692

commit v4 on v3

--- a/solution.py
+++ b/solution.py
@@ -14,6 +14,7 @@
 GROUPS = 4
 R = E // CH
 GPC = GROUPS // CH
+ORDER = (0, 1, 2, 3)
 COLS = D // 128
 SLAB = 12
 F32, BF16 = jnp.float32, jnp.bfloat16
@@ -50,23 +51,21 @@
     right = ((xs + 1) % 4) * 2 + core
     left = ((xs + 3) % 4) * 2 + core
     far = ((xs + 2) % 4) * 2 + core
-    by_dy = [((y + dy) % 4) * 16 for dy in (3, 2, 1, 0)]
-    by_minus_dy = [((y + 4 - dy) % 4) * 16 for dy in (3, 2, 1, 0)]
-
-    def dz_of(k, j):
-        odd = j % 2
-        return (1 - 2 * odd) * (8 - k + (j // 2) * (2 * k - 7)) + odd + 16
-
     def each_row(k, do):
-        def four(j, c):
-            for n in range(4):
-                do(16 * k + 4 * j + n, n, dz_of(k, j))
+        g = ORDER[k]
+
+        def body(n, c):
+            for j, dz in enumerate((8 - g, g - 7, g + 1, -g)):
+                do(16 * k + 4 * j + n, 3 - n, dz)
             return c
 
-        lax.fori_loop(0, 3 if k == 0 else 4, four, 0)
-        if k == 0:
-            for n in range(3):
-                do(12 + n, n, 16)
+        lax.fori_loop(0, 4, body, 0)
+
+    def other_core(e):
+        return {"section": partner, "expert": e}
+
+    def at_offset(dy, dz):
+        return ((y + dy + 4) % 4) * 16 + (z + dz + 16) % 16
 
     loads = [
         pltpu.make_async_copy(src, dst, load_sem.at[i])
@@ -80,11 +79,11 @@
     barrier = pltpu.get_barrier_semaphore()
 
     def greet(e):
-        pl.semaphore_signal(barrier, inc=1, device_id={"expert": e}, device_id_type=MESH)
+        pl.semaphore_signal(barrier, inc=1, device_id=other_core(e), device_id_type=MESH)
 
     for g in range(GROUPS):
-        each_row(g, lambda i, n, dz: greet(by_dy[n] + (z + dz) % 16))
-    for peer in (left, right, far, partner):
+        each_row(g, lambda i, dy, dz: greet(at_offset(dy, dz)))
+    for peer in (left, right, far):
         pl.semaphore_signal(barrier, inc=1, device_id={"section": peer}, device_id_type=MESH)
 
     for c in loads[:3]:
@@ -104,16 +103,15 @@
     slot_in = lax.dot_general(dispatch, normed[...], (((0,), (0,)), ((), ())), preferred_element_type=F32)
     to_slabs(slot_in, wide, send_a, E)
 
-    pl.semaphore_wait(barrier, E - 1 + 4)
+    pl.semaphore_wait(barrier, E + 3)
 
     def send_row(k, i, e):
         pltpu.make_async_remote_copy(
-            send_a.at[e], recv_a.at[i], a2a_s.at[0], a_r.at[k], device_id={"expert": e}, device_id_type=MESH
+            send_a.at[e], recv_a.at[i], a2a_s.at[0], a_r.at[k], device_id=other_core(e), device_id_type=MESH
         ).start()
 
     for g in range(GROUPS):
-        each_row(g, lambda i, n, dz, g=g: send_row(g // GPC, i, by_dy[n] + (z + dz) % 16))
-    recv_a[15] = send_a[me]
+        each_row(g, lambda i, dy, dz, g=g: send_row(g // GPC, i, at_offset(dy, dz)))
     for c in loads[3:]:
         c.wait()
     for i in range(FH // 128):
@@ -147,7 +145,7 @@
         sums.append([c_copy(k, 1, FAR, 2, far), c_copy(k, 2, LEFT, 0, left), c_copy(k, 3, RIGHT, 1, right)])
 
     def s0(k):
-        slabs_in(recv_a, R if k else R - 1, a_r.at[k])
+        slabs_in(recv_a, R, a_r.at[k])
         from_slabs(recv_a.at[pl.ds(R * k, R)], wide_in.at[k], gat.at[k, pl.ds(0, R)], R)
         for c in hops[k]:
             c.start()
@@ -185,25 +183,27 @@
 
         def return_row(i, e):
             pltpu.make_async_remote_copy(
-                send_d.at[i], recv_d.at[me], a2a_s.at[1], d_r.at[0], device_id={"expert": e}, device_id_type=MESH
+                send_d.at[i], recv_d.at[me], a2a_s.at[1], d_r.at[0], device_id=other_core(e), device_id_type=MESH
             ).start()
 
         for g in range(GPC * k, GPC * (k + 1)):
-            each_row(g, lambda i, n, dz: return_row(i, by_minus_dy[n] + (z + 32 - dz) % 16))
-        if k == 0:
-            recv_d[me] = send_d[15]
+            each_row(g, lambda i, dy, dz: return_row(i, at_offset(-dy, -dz)))
 
     stages = (s0, s1, s2, s3, s4)
-    order = (0, 1, 10, 2, 20, 11, 3, 30, 21, 12, 31, 22, 13, 40, 32, 23, 41, 33, 42, 43)
+    order = (0, 1, 10, 2, 20, 11, 3, 30, 21, 12, 31, 22, 13, 32, 23, 40, 33, 41, 42, 43)
     for step in order:
         stages[step // 10](step % 10)
 
     for c in to_other + on + pair + sum(hops + sums, []):
         c.wait_send()
-    slabs_in(send_a, E - 1, a2a_s.at[0])
-    slabs_in(send_d, E - 1, a2a_s.at[1])
-    slabs_in(recv_d, E - 1, d_r.at[0])
+    slabs_in(send_a, E, a2a_s.at[0])
+    slabs_in(send_d, E, a2a_s.at[1])
+    slabs_in(recv_d, E, d_r.at[0])
     from_slabs(recv_d, wide, back, E)
+
+
+def in_hbm(array):
+    return pltpu.with_memory_space_constraint(array, pltpu.HBM)
 
 
 def exchange(images, norm_gain, slot_map, logit_scale, up_weight, down_weight):
@@ -225,8 +225,8 @@
             pltpu.VMEM((CH, 3, R, D), BF16),
             dma((5,)), dma((2,)), dma((CH,)), dma((1,)), dma((CH, 5)), dma((CH, 5)), dma((CH, 4)), dma((CH, 4)),
         ],
-        compiler_params=pltpu.CompilerParams(collective_id=0, has_side_effects=True, vmem_limit_bytes=56 * 1024 * 1024),
-    )(images, norm_gain, slot_map.T, logit_scale, up_weight, down_weight)
+        compiler_params=pltpu.CompilerParams(collective_id=0, has_side_effects=True, vmem_limit_bytes=52 * 1024 * 1024),
+    )(in_hbm(images), in_hbm(norm_gain), in_hbm(slot_map.T), logit_scale, in_hbm(up_weight), in_hbm(down_weight))
 
 
 def local(images, norm_gain, slot_map, logit_scale, up_weight, down_weight):

time: 61.1 us -> 59.8 us (0.979)
  matrix products: 2.15 us -> 1.19 us
    dot_general x1, matrix products: 2.15 us -> 1.19 us  [local(): mixed = jnp.einsum('te,ed->td', comb, back, preferred_element_type=F32)]
where the time goes in v4:
time: 59.8 us; the launch traced here: 59.7 us
  Pallas kernels  57.8 us (97%)
  matrix products  1.19 us (2%)
  between operations  0.68 us (1%)
    pallas_call x1, Pallas kernels, exchange(): pl.pallas_call(kernel, out_shape=(jax.ShapeDtypeStruct((E, D), BF16), jax...  57.8 us

profile of v4, /device:TPU:1, one launch (start us, length us, event | category | flops | bytes accessed | tf_op | source)
XLA Modules:
  0.0 59.7 jit_solution(2153938872387044278)
XLA Ops:
  0.7 0.0 copy-start
  0.7 57.8 %shard_map.64 = (bf16[64,1408]{1,0:T(8,128)(2,1)S(1)}, bf16[256,64]{1,0:T(8,128)(2,1)S(1)}) custom-call(bf16[1,256,1408]{2,1,0:T(8,128)(2,1)} %images.1, bf16[1408]{0:T(1024)(128)(2,1)} %gain.1, bf16[64,1408]{1,0:T(8,128)(2,1)} %bitcast.9, f32[1]{0:T(128)S(6)} %copy.7.scale, bf16[1,640,1408]{2,1,0:T(8,128)(2,1)} %up.1, bf16[1,640,1408]{2,1,0:T(8,128)(2,1)} %down.1), custom_call_target="tpu_custom_call" | custom-call | tf_op jit(solution)/shard_map/pallas_call | solution.py:212
  58.5 0.0 copy-done
  58.5 1.2 %fusion.1 = bf16[1,256,1408]{2,1,0:T(8,128)(2,1)} fusion(bf16[256,64]{1,0:T(8,128)(2,1)S(1)} %get-tuple-element.7, bf16[64,1408]{1,0:T(8,128)(2,1)S(1)} %get-tuple-element.8, bf16[1,256,1408]{2,1,0:T(8,128)(2,1)S(1)} %copy-done), kind=kOutput, calls=%fused_computation.2 | convolution fusion | flops 47218688 | bytes 1654784 | tf_op jit(solution)/shard_map/te,ed->td/dot_general | solution.py:234
Async XLA Ops:
  0.7 57.9 %copy-start = (bf16[1,256,1408]{2,1,0:T(8,128)(2,1)S(1)}, bf16[1,256,1408]{2,1,0:T(8,128)(2,1)}, u32[]{:S(2)}) copy-start(bf16[1,256,1408]{2,1,0:T(8,128)(2,1)} %images.1) | copy-start | bytes 2162692

commit v5 on v4

--- a/solution.py
+++ b/solution.py
@@ -16,7 +16,7 @@
 GPC = GROUPS // CH
 ORDER = (0, 1, 2, 3)
 COLS = D // 128
-SLAB = 12
+SLAB = 11
 F32, BF16 = jnp.float32, jnp.bfloat16
 MESH = pl.DeviceIdType.MESH
 OWN, LEFT, RIGHT, FAR = 0, 1, 2, 3
@@ -140,7 +140,10 @@
             b_copy(k, 2, rows(k, OWN), rows(k, RIGHT), left),
         ])
         to_other.append(b_copy(k, 3, rows(k, OWN), rows(k, OWN, 1, 1), partner))
-        on.append(b_copy(k, 4, rows(k, LEFT, 3), rows(k, LEFT, 3, 1), partner))
+        on.append([
+            b_copy(k, 4, rows(k, LEFT, 2), rows(k, LEFT, 2, 1), partner),
+            b_copy(k, 5, rows(k, FAR), rows(k, FAR, 1, 1), partner),
+        ])
         pair.append(section_copy(p_out.at[k], p_in.at[k], cs.at[k, 0], cr.at[k, 0], partner))
         sums.append([c_copy(k, 1, FAR, 2, far), c_copy(k, 2, LEFT, 0, left), c_copy(k, 3, RIGHT, 1, right)])
 
@@ -152,13 +155,16 @@
         to_other[k].start()
 
     def s1(k):
-        for c in hops[k]:
-            c.wait_recv()
-        on[k].start()
+        hops[k][1].wait_recv()
+        hops[k][2].wait_recv()
+        on[k][0].start()
+        hops[k][0].wait_recv()
+        on[k][1].start()
 
     def s2(k):
         to_other[k].wait_recv()
-        on[k].wait_recv()
+        for c in on[k]:
+            c.wait_recv()
         up_out = jnp.dot(gat[k], up_t[...], preferred_element_type=F32)
         hid[k] = jax.nn.gelu(up_out).astype(BF16)
         part = jnp.dot(hid[k], down_v[...], preferred_element_type=F32)
@@ -190,11 +196,11 @@
             each_row(g, lambda i, dy, dz: return_row(i, at_offset(-dy, -dz)))
 
     stages = (s0, s1, s2, s3, s4)
-    order = (0, 1, 10, 2, 20, 11, 3, 30, 21, 12, 31, 22, 13, 32, 23, 40, 33, 41, 42, 43)
+    order = (0, 1, 10, 2, 20, 11, 30, 3, 21, 31, 12, 22, 40, 13, 32, 23, 41, 33, 42, 43)
     for step in order:
         stages[step // 10](step % 10)
 
-    for c in to_other + on + pair + sum(hops + sums, []):
+    for c in to_other + pair + sum(hops + on + sums, []):
         c.wait_send()
     slabs_in(send_a, E, a2a_s.at[0])
     slabs_in(send_d, E, a2a_s.at[1])
@@ -223,7 +229,7 @@
             pltpu.VMEM((CH, 8 * R, D), BF16), pltpu.VMEM((CH, 8 * R, FH), BF16), pltpu.VMEM((CH, 4 * R, D), F32),
             pltpu.VMEM((CH, 4 * R, D), BF16), pltpu.VMEM((CH, 4 * R, D), BF16), pltpu.VMEM((CH, 4 * R, D), BF16),
             pltpu.VMEM((CH, 3, R, D), BF16),
-            dma((5,)), dma((2,)), dma((CH,)), dma((1,)), dma((CH, 5)), dma((CH, 5)), dma((CH, 4)), dma((CH, 4)),
+            dma((5,)), dma((2,)), dma((CH,)), dma((1,)), dma((CH, 6)), dma((CH, 6)), dma((CH, 4)), dma((CH, 4)),
         ],
         compiler_params=pltpu.CompilerParams(collective_id=0, has_side_effects=True, vmem_limit_bytes=52 * 1024 * 1024),
     )(in_hbm(images), in_hbm(norm_gain), in_hbm(slot_map.T), logit_scale, in_hbm(up_weight), in_hbm(down_weight))

time: 59.8 us -> 59.7 us (level)
  no operation moved by 1% of the time
where the time goes in v5:
time: 59.7 us; the launch traced here: 59.6 us
  Pallas kernels  57.7 us (97%)
  matrix products  1.19 us (2%)
  between operations  0.68 us (1%)
    pallas_call x1, Pallas kernels, exchange(): pl.pallas_call(kernel, out_shape=(jax.ShapeDtypeStruct((E, D), BF16), jax...  57.7 us

profile of v5, /device:TPU:1, one launch (start us, length us, event | category | flops | bytes accessed | tf_op | source)
XLA Modules:
  0.0 59.6 jit_solution(9381369724570759663)
XLA Ops:
  0.7 0.0 copy-start
  0.7 57.7 %shard_map.64 = (bf16[64,1408]{1,0:T(8,128)(2,1)S(1)}, bf16[256,64]{1,0:T(8,128)(2,1)S(1)}) custom-call(bf16[1,256,1408]{2,1,0:T(8,128)(2,1)} %images.1, bf16[1408]{0:T(1024)(128)(2,1)} %gain.1, bf16[64,1408]{1,0:T(8,128)(2,1)} %bitcast.9, f32[1]{0:T(128)S(6)} %copy.7.scale, bf16[1,640,1408]{2,1,0:T(8,128)(2,1)} %up.1, bf16[1,640,1408]{2,1,0:T(8,128)(2,1)} %down.1), custom_call_target="tpu_custom_call" | custom-call | tf_op jit(solution)/shard_map/pallas_call | solution.py:218
  58.4 0.0 copy-done
  58.4 1.2 %fusion.1 = bf16[1,256,1408]{2,1,0:T(8,128)(2,1)} fusion(bf16[256,64]{1,0:T(8,128)(2,1)S(1)} %get-tuple-element.7, bf16[64,1408]{1,0:T(8,128)(2,1)S(1)} %get-tuple-element.8, bf16[1,256,1408]{2,1,0:T(8,128)(2,1)S(1)} %copy-done), kind=kOutput, calls=%fused_computation.2 | convolution fusion | flops 47218688 | bytes 1654784 | tf_op jit(solution)/shard_map/te,ed->td/dot_general | solution.py:240
Async XLA Ops:
  0.7 57.7 %copy-start = (bf16[1,256,1408]{2,1,0:T(8,128)(2,1)S(1)}, bf16[1,256,1408]{2,1,0:T(8,128)(2,1)}, u32[]{:S(2)}) copy-start(bf16[1,256,1408]{2,1,0:T(8,128)(2,1)} %images.1) | copy-start | bytes 2162692

commit v6 on v5

--- a/solution.py
+++ b/solution.py
@@ -48,9 +48,9 @@
     xs, core = sec // 2, sec % 2
     y, z = me // 16, me % 16
     partner = sec + 1 - 2 * core
-    right = ((xs + 1) % 4) * 2 + core
-    left = ((xs + 3) % 4) * 2 + core
-    far = ((xs + 2) % 4) * 2 + core
+    right = ((xs + 1) % 4) * 2 + 1 - core
+    left = ((xs + 3) % 4) * 2 + 1 - core
+    far = ((xs + 2) % 4) * 2 + 1 - core
     def each_row(k, do):
         g = ORDER[k]
 

time: 59.7 us -> 59.9 us (level)
  no operation moved by 1% of the time
where the time goes in v6:
time: 59.9 us; the launch traced here: 59.8 us
  Pallas kernels  57.9 us (97%)
  matrix products  1.19 us (2%)
  between operations  0.68 us (1%)
    pallas_call x1, Pallas kernels, exchange(): pl.pallas_call(kernel, out_shape=(jax.ShapeDtypeStruct((E, D), BF16), jax...  57.9 us

profile of v6, /device:TPU:1, one launch (start us, length us, event | category | flops | bytes accessed | tf_op | source)
XLA Modules:
  0.0 59.8 jit_solution(15897131762284203989)
XLA Ops:
  0.7 0.0 copy-start
  0.7 57.9 %shard_map.64 = (bf16[64,1408]{1,0:T(8,128)(2,1)S(1)}, bf16[256,64]{1,0:T(8,128)(2,1)S(1)}) custom-call(bf16[1,256,1408]{2,1,0:T(8,128)(2,1)} %images.1, bf16[1408]{0:T(1024)(128)(2,1)} %gain.1, bf16[64,1408]{1,0:T(8,128)(2,1)} %bitcast.9, f32[1]{0:T(128)S(6)} %copy.7.scale, bf16[1,640,1408]{2,1,0:T(8,128)(2,1)} %up.1, bf16[1,640,1408]{2,1,0:T(8,128)(2,1)} %down.1), custom_call_target="tpu_custom_call" | custom-call | tf_op jit(solution)/shard_map/pallas_call | solution.py:218
  58.6 0.0 copy-done
  58.6 1.2 %fusion.1 = bf16[1,256,1408]{2,1,0:T(8,128)(2,1)} fusion(bf16[256,64]{1,0:T(8,128)(2,1)S(1)} %get-tuple-element.7, bf16[64,1408]{1,0:T(8,128)(2,1)S(1)} %get-tuple-element.8, bf16[1,256,1408]{2,1,0:T(8,128)(2,1)S(1)} %copy-done), kind=kOutput, calls=%fused_computation.2 | convolution fusion | flops 47218688 | bytes 1654784 | tf_op jit(solution)/shard_map/te,ed->td/dot_general | solution.py:240
Async XLA Ops:
  0.7 58.0 %copy-start = (bf16[1,256,1408]{2,1,0:T(8,128)(2,1)S(1)}, bf16[1,256,1408]{2,1,0:T(8,128)(2,1)}, u32[]{:S(2)}) copy-start(bf16[1,256,1408]{2,1,0:T(8,128)(2,1)} %images.1) | copy-start | bytes 2162692
